TPU v7x, 32 devices: a whole 2x2x4 slice. The times are simulated.
32 devices in a mesh: cfg: 2 (over y), seq: 8 (over z, core), tp: 2 (over x).
Axes of the slice: x: 2, y: 2, z: 4, core: 2. Of those that a mesh axis runs over, the one named last changes fastest.
Arguments:
- queries: bfloat16 [2, 3840, 5120], P('cfg', 'seq', 'tp'), may hold values from -5 to 5
- keys: bfloat16 [2, 3840, 5120], P('cfg', 'seq', 'tp'), may hold values from -5 to 5
- values: bfloat16 [2, 3840, 5120], P('cfg', 'seq', 'tp'), may hold values from -5 to 5
- text_keys: bfloat16 [2, 512, 5120], P('cfg', None, 'tp'), may hold values from -7.5 to 7.5
- text_values: bfloat16 [2, 512, 5120], P('cfg', None, 'tp'), may hold values from -5 to 5
- prompt_lengths: int32 [2], P('cfg'), may hold values from 64 to 512
- frame_counts: int32 [8], P('seq'), may hold values from 240 to 480
- out_weight: bfloat16 [5120, 5120], P('tp'), may hold values from -0.5 to 0.5
Outputs:
- velocity: bfloat16 [3840, 5120], P('seq', ('tp', 'cfg'))
All inputs are finite; a program needn't handle non-finite values.
Results may differ from a plain program's by a relative error of at most 0.015.
Values may be sent and summed in bfloat16 or wider, within the bound.
A program may use at most 320 MiB of HBM per device.

v0:
```python
import jax
import jax.numpy as jnp
from jax import lax
from jax.sharding import PartitionSpec as P

HEAD_DIM = 128
FRAME_SLOTS = 480
GUIDANCE = 5.0
RESCALE = 0.7
NEGATIVE = -1e30


def frame_valid(positions, counts_table):
    frame_index = positions // FRAME_SLOTS
    slot_index = positions % FRAME_SLOTS
    frame_ids = jnp.arange(counts_table.shape[0], dtype=jnp.int32)
    frame_limit = jnp.sum(
        jnp.where(frame_index[:, None] == frame_ids[None, :], counts_table[None, :], 0), axis=1
    )
    return slot_index < frame_limit


def attend_block(carry, key_rows, value_rows, query_heads, key_mask):
    row_max, weight_sum, mixed_sum = carry
    head_count = query_heads.shape[1]
    key_heads = key_rows.reshape(key_rows.shape[0], head_count, HEAD_DIM)
    value_heads = value_rows.reshape(value_rows.shape[0], head_count, HEAD_DIM)
    scores = jnp.einsum(
        "qhd,khd->hqk", query_heads, key_heads, preferred_element_type=jnp.float32
    ) * HEAD_DIM ** (-0.5)
    scores = jnp.where(key_mask[None, None, :], scores, NEGATIVE)
    new_max = jnp.maximum(row_max, jnp.max(scores, axis=2))
    shrink = jnp.exp(row_max - new_max)
    weights = jnp.exp(scores - new_max[:, :, None])
    weight_sum = weight_sum * shrink + jnp.sum(weights, axis=2)
    mixed_sum = mixed_sum * shrink[:, :, None] + jnp.einsum(
        "hqk,khd->hqd",
        weights.astype(jnp.bfloat16),
        value_heads,
        preferred_element_type=jnp.float32,
    )
    return (new_max, weight_sum, mixed_sum)


def body(queries, keys, values, text_keys, text_values, prompt_lengths, frame_counts, out_weight):
    row_count = queries.shape[1]
    head_cols = queries.shape[2]
    head_count = head_cols // HEAD_DIM
    all_counts = lax.all_gather(frame_counts, "seq", axis=0, tiled=True)
    query_heads = queries[0].reshape(row_count, head_count, HEAD_DIM)
    text_mask = jnp.arange(text_keys.shape[1], dtype=jnp.int32) < prompt_lengths[0]
    empty_state = (
        jnp.full((head_count, row_count), NEGATIVE, jnp.float32),
        jnp.zeros((head_count, row_count), jnp.float32),
        jnp.zeros((head_count, row_count, HEAD_DIM), jnp.float32),
    )
    text_state = attend_block(empty_state, text_keys[0], text_values[0], query_heads, text_mask)
    key_rows = lax.all_gather(keys[0], "seq", axis=0, tiled=True)
    value_rows = lax.all_gather(values[0], "seq", axis=0, tiled=True)
    positions = jnp.arange(key_rows.shape[0], dtype=jnp.int32)
    row_max, weight_sum, mixed_sum = attend_block(
        text_state, key_rows, value_rows, query_heads, frame_valid(positions, all_counts)
    )
    attended = (
        jnp.transpose(mixed_sum / weight_sum[:, :, None], (1, 0, 2))
        .reshape(row_count, head_cols)
        .astype(jnp.bfloat16)
    )
    projected = (
        lax.psum_scatter(
            lax.dot_general(
                out_weight, attended, (((0,), (1,)), ((), ())), preferred_element_type=jnp.float32
            ).astype(jnp.bfloat16),
            "tp",
            scatter_dimension=0,
            tiled=True,
        )
        .astype(jnp.float32)
        .T
    )
    branch = projected.astype(jnp.bfloat16)[None]
    half_cols = head_cols // 2
    gathered = lax.all_gather(branch, "cfg", axis=0, tiled=True)
    paired = lax.dynamic_slice_in_dim(gathered, lax.axis_index("cfg") * half_cols, half_cols, 2)
    conditional = paired[0].astype(jnp.float32)
    unconditional = paired[1].astype(jnp.float32)
    guided = unconditional + GUIDANCE * (conditional - unconditional)
    token_weights = frame_valid(jnp.arange(row_count, dtype=jnp.int32), frame_counts).astype(
        jnp.float32
    )

    def local_sum(field_rows):
        return jnp.dot(token_weights, field_rows, precision=lax.Precision.HIGHEST)

    guided_sum, guided_square, cond_sum, cond_square = lax.psum(
        (
            local_sum(guided),
            local_sum(guided * guided),
            local_sum(conditional),
            local_sum(conditional * conditional),
        ),
        "seq",
    )
    valid_total = jnp.sum(all_counts).astype(jnp.float32)
    guided_mean = guided_sum / valid_total
    guided_var = guided_square / valid_total - guided_mean * guided_mean
    cond_mean = cond_sum / valid_total
    cond_var = cond_square / valid_total - cond_mean * cond_mean
    std_ratio = jnp.sqrt((cond_var + 1.0) / (guided_var + 1.0))
    factor = RESCALE * std_ratio + (1.0 - RESCALE)
    return (guided_mean + (guided - guided_mean) * factor).astype(jnp.bfloat16)


def solution(mesh):
    placed = (
        P("cfg", "seq", "tp"),
        P("cfg", "seq", "tp"),
        P("cfg", "seq", "tp"),
        P("cfg", None, "tp"),
        P("cfg", None, "tp"),
        P("cfg"),
        P("seq"),
        P("tp", None),
    )
    return jax.shard_map(
        body, mesh=mesh, in_specs=placed, out_specs=P("seq", ("tp", "cfg")), check_vma=False
    )
```

profile of v0, /device:TPU:0, one launch (start us, length us, event | category | flops | bytes accessed | tf_op | source)
XLA Modules:
  0.0 636.8 jit_solution(17651519796824386608)
XLA Ops:
  6.5 0.0 copy-start.4
  6.5 0.0 all-gather.7.cloned.1.call-start
  6.5 0.7 all-gather.7.cloned.1.call-update
  7.3 0.0 all-gather.9.cloned.1.call-start
  7.3 0.7 all-gather.9.cloned.1.call-update
  8.0 0.0 reduce-scatter.2.cloned.1.call-start
  8.7 0.0 copy-done.4
  8.7 0.6 dynamic-slice
  9.3 0.7 dynamic-update-slice
  10.0 10.6 %all-reduce = s32[8]{0:T(128)S(1)} all-reduce(s32[8]{0:T(128)S(1)} %dynamic-update-slice), channel_id=1, replica_groups=mesh['cfg'=2,'seq'=8,'tp'=2] {'seq'}, use_global_device_ids=true, to_apply=%add | all-reduce | flops 8 | bytes 64
  20.6 0.0 copy-start.2
  20.6 3.2 copy.37
  24.4 4.5 copy.38
  28.9 4.4 copy.41
  33.4 0.0 copy-done.2
  33.4 0.1 select_reduce_fusion
  33.5 12.2 %fusion.6 = (f32[20,480]{1,0:T(8,128)S(1)}, f32[20,480,512]{2,1,0:T(8,128)}) fusion(pred[512]{0:T(512)(128)(4,1)S(1)} %iota_compare_fusion.2, bf16[480,20,128]{0,2,1:T(8,128)(2,1)S(1)} %bitcast.86, bf16[512,20,128]{0,2,1:T(8,128)(2,1)} %bitcast.89), kind=kOutput, calls=%fused_computation.9 | convolution fusion | flops 1273027200 | bytes 24778752 | tf_op jit(solution)/shard_map/qhd,khd->hqk/dot_general | solution.py:28
  45.7 140.8 %all-gather.7.cloned.1.call-done = bf16[1,3840,2560]{2,1,0:T(8,128)(2,1)} async-done(((bf16[1,480,2560]{2,1,0:T(8,128)(2,1)}), bf16[1,3840,2560]{2,1,0:T(8,128)(2,1)}) %all-gather.7.cloned.1.call-update) | async-done | bytes 19660816 | tf_op jit(solution)/shard_map/all_gather | solution.py:58
  186.5 25.5 %copy.43 = bf16[1,3840,2560]{1,2,0:T(8,128)(2,1)} copy(bf16[1,3840,2560]{2,1,0:T(8,128)(2,1)} %all-gather.7.cloned.1.call-done) | data formatting | bytes 39321600 | tf_op jit(solution)/shard_map/all_gather | solution.py:58
  211.9 58.6 %fusion = (f32[20,480]{1,0:T(8,128)S(1)}, f32[20,480,3840]{2,1,0:T(8,128)}) fusion(pred[3840]{0:T(1024)(128)(4,1)S(1)} %fusion.37, bf16[480,20,128]{0,2,1:T(8,128)(2,1)S(1)} %bitcast.87, bf16[3840,20,128]{0,2,1:T(8,128)(2,1)} %bitcast.85), kind=kOutput, calls=%fused_computation.2 | convolution fusion | flops 9547766784 | bytes 169616640 | tf_op jit(solution)/shard_map/qhd,khd->hqk/dot_general | solution.py:28
  270.5 9.7 %fusion.7 = f32[20,480]{1,0:T(8,128)S(1)} fusion(f32[20,480,512]{2,1,0:T(8,128)} %get-tuple-element.19, f32[20,480]{1,0:T(8,128)S(1)} %get-tuple-element.13, pred[512]{0:T(512)(128)(4,1)S(1)} %iota_compare_fusion.2), kind=kLoop, calls=%fused_computation.10 | loop fusion | flops 19651200 | bytes 19738112 | tf_op jit(solution)/shard_map/reduce_sum | solution.py:35
  280.2 0.0 copy-start.1
  280.2 45.5 %fusion.1 = f32[20,480]{1,0:T(8,128)S(1)} fusion(f32[20,480,3840]{2,1,0:T(8,128)} %get-tuple-element.17, f32[20,480]{1,0:T(8,128)S(1)} %get-tuple-element.12, pred[3840]{0:T(1024)(128)(4,1)S(1)} %fusion.37), kind=kLoop, calls=%fused_computation.3 | loop fusion | flops 147446400 | bytes 147536640 | tf_op jit(solution)/shard_map/reduce_sum | solution.py:35
  325.8 0.0 copy-done.1
  325.8 10.5 %fusion.9 = f32[20,480,128]{2,1,0:T(8,128)} fusion(bf16[512,20,128]{0,2,1:T(8,128)(2,1)S(1)} %bitcast.95, f32[20,480,512]{2,1,0:T(8,128)} %get-tuple-element.19, f32[20,480]{1,0:T(8,128)S(1)} %get-tuple-element.13, pred[512]{0:T(512)(128)(4,1)S(1)} %iota_compare_fusion.2), kind=kOutput, calls=%fused_computation.12 | convolution fusion | flops 1277952000 | bytes 27236352 | tf_op jit(solution)/shard_map/hqk,khd->hqd/dot_general | solution.py:36
  336.2 24.8 %all-gather.9.cloned.1.call-done = bf16[1,3840,2560]{2,1,0:T(8,128)(2,1)} async-done(((bf16[1,480,2560]{2,1,0:T(8,128)(2,1)}), bf16[1,3840,2560]{2,1,0:T(8,128)(2,1)}) %all-gather.9.cloned.1.call-update) | async-done | bytes 19660816 | tf_op jit(solution)/shard_map/all_gather | solution.py:59
  361.0 24.1 %copy.46 = bf16[1,3840,2560]{1,2,0:T(8,128)(2,1)} copy(bf16[1,3840,2560]{2,1,0:T(8,128)(2,1)} %all-gather.9.cloned.1.call-done) | data formatting | bytes 39321600 | tf_op jit(solution)/shard_map/all_gather | solution.py:59
  385.1 55.6 %fusion.17 = bf16[480,20,128]{2,0,1:T(8,128)(2,1)} fusion(f32[20,480,128]{2,1,0:T(8,128)} %fusion.9, f32[480,20]{0,1:T(8,128)S(1)} %get-tuple-element.9, f32[480,20]{0,1:T(8,128)S(1)} %get-tuple-element.10, f32[480,20]{0,1:T(8,128)S(1)} %get-tuple-element.11, bf16[3840,20,128]{0,2,1:T(8,128)(2,1)} %bitcast.88, f32[20,480,3840]{2,1,0:T(8,128)} %get-tuple-element.17, ...), kind=kOutput, calls=%fused_computation.21 | convolution fusion | flops 9590784000 | bytes 174647040 | tf_op jit(solution)/shard_map/hqk,khd->hqd/dot_general | solution.py:36
  440.7 2.9 copy.48
  443.6 19.5 %fusion.15 = bf16[5120,480]{0,1:T(8,128)(2,1)} fusion(bf16[480,2560]{0,1:T(8,128)(2,1)S(1)} %bitcast.96, bf16[2560,5120]{1,0:T(8,128)(2,1)} %param.15), kind=kOutput, calls=%fused_computation.18 | convolution fusion | flops 12585369600 | bytes 33587200 | tf_op jit(solution)/shard_map/dot_general | solution.py:71
  463.2 0.0 copy-start.3
  463.2 0.0 reduce-scatter.2.cloned.1.call-update
  463.2 0.0 all-gather.11.cloned.1.call-start
  463.2 60.5 %reduce-scatter.2.cloned.1.call-done = bf16[2560,480]{0,1:T(8,128)(2,1)} async-done(((bf16[5120,480]{0,1:T(8,128)(2,1)}), bf16[2560,480]{0,1:T(8,128)(2,1)}) %reduce-scatter.2.cloned.1.call-update) | async-done | bytes 2457616 | tf_op jit(solution)/shard_map/reduce_scatter | solution.py:70
  523.7 0.0 all-gather.11.cloned.1.call-update
  523.7 0.0 copy-done.3
  523.8 0.7 reduce_sum.49
  525.1 65.0 %all-gather.11.cloned.1.call-done = bf16[960,2560]{1,0:T(8,128)(2,1)} async-done(((bf16[480,2560]{1,0:T(8,128)(2,1)}), bf16[960,2560]{1,0:T(8,128)(2,1)}) %all-gather.11.cloned.1.call-update) | async-done | bytes 4915216 | tf_op jit(solution)/shard_map/all_gather | solution.py:83
  590.0 0.0 copy-start
  590.0 1.7 convolution_reduce_fusion
  591.7 2.4 fusion.28
  594.2 2.9 fusion.29
  597.1 0.0 copy-done
  597.2 1.4 fusion.30
  598.5 28.4 %all-reduce.1 = (f32[1280]{0:T(1024)S(1)}, f32[1280]{0:T(1024)S(1)}, f32[1280]{0:T(1024)S(1)}, f32[1280]{0:T(1024)S(1)}) all-reduce(f32[1280]{0:T(1024)S(1)} %fusion.30, f32[1280]{0:T(1024)S(1)} %convolution_reduce_fusion, f32[1280]{0:T(1024)S(1)} %fusion.28, f32[1280]{0:T(1024)S(1)} %fusion.29), channel_id=1, replica_groups=mesh['cfg'=2,'seq'=8,'tp'=2] {'seq'}, use_global_device_ids=true, to_apply=%region_10.11 | all-reduce | flops 5120 | bytes 40960 | tf_op jit(solution)/shard_map/psum | solution.py:95
  626.9 3.4 add_convert_fusion
  (9 shorter events, 0.1 us)
Async XLA Ops:
  6.5 2.2 copy-start.4
  6.5 179.9 %all-gather.7.cloned.1.call-start = ((), (), s32[]{:S(2)}) async-start(), calls=%async_computation.2 | async-start | bytes 22118400 | tf_op jit(solution)/shard_map/all_gather | solution.py:58
  7.3 353.8 %all-gather.9.cloned.1.call-start = ((), (), s32[]{:S(2)}) async-start(), calls=%async_computation.3 | async-start | bytes 22118400 | tf_op jit(solution)/shard_map/all_gather | solution.py:59
  8.0 515.7 %reduce-scatter.2.cloned.1.call-start = ((), (), s32[]{:S(2)}) async-start(), calls=%async_computation.1 | async-start | bytes 7372800 | tf_op jit(solution)/shard_map/reduce_scatter | solution.py:70
  20.6 12.8 %copy-start.2 = (s32[8]{0:T(128)}, s32[8]{0:T(128)S(1)}, u32[]{:S(2)}) copy-start(s32[8]{0:T(128)S(1)} %all-reduce) | copy-start | bytes 100
  280.2 45.6 %copy-start.1 = (bf16[1,512,2560]{1,2,0:T(8,128)(2,1)S(1)}, bf16[1,512,2560]{1,2,0:T(8,128)(2,1)}, u32[]{:S(2)}) copy-start(bf16[1,512,2560]{1,2,0:T(8,128)(2,1)} %copy.41) | copy-start | bytes 7864324
  463.2 60.6 %copy-start.3 = (s32[8]{0:T(128)S(1)}, s32[8]{0:T(128)}, u32[]{:S(2)}) copy-start(s32[8]{0:T(128)} %copy-done.2) | copy-start | bytes 100
  463.2 126.8 %all-gather.11.cloned.1.call-start = ((), (), s32[]{:S(2)}) async-start(), calls=%async_computation.4 | async-start | bytes 7372800 | tf_op jit(solution)/shard_map/all_gather | solution.py:83
  590.0 7.1 %copy-start = (bf16[960,2560]{1,0:T(8,128)(2,1)S(1)}, bf16[960,2560]{1,0:T(8,128)(2,1)}, u32[]{:S(2)}) copy-start(bf16[960,2560]{1,0:T(8,128)(2,1)} %all-gather.11.cloned.1.call-done) | copy-start | bytes 14745604
Sparse Core Ops, SparseCore 0:
  9.0 177.4 all-gather.6
  188.1 172.8 all-gather.8
  463.3 60.3 reduce-scatter.1
  525.1 64.8 all-gather.10
where the time goes:
time: 639 us; the launch traced here: 637 us
  waiting for transfers between devices  292 us (46%)
  matrix products  165 us (26%)
  local copies, waits for them, and re-layouts  65.8 us (10%)
  other arithmetic  59.5 us (9%)
  blocking collectives  39 us (6%)
  between operations  15.2 us (2%)
    all_gather x1, waiting for transfers between devices, body(): key_rows = lax.all_gather(keys[0], 'seq', axis=0, tiled=True)  141 us
    dot_general x2, matrix products, attend_block(): jnp.einsum('qhd,khd->hqk', query_heads, key_heads, preferred_element_type...  70.7 us
    dot_general x2, matrix products, attend_block(): jnp.einsum('hqk,khd->hqd', weights.astype(jnp.bfloat16), value_heads, pre...  66.1 us
    all_gather x1, waiting for transfers between devices, body(): gathered = lax.all_gather(branch, 'cfg', axis=0, tiled=True)  65 us
    reduce_scatter x1, waiting for transfers between devices, body(): lax.psum_scatter(lax.dot_general(out_weight, attended, (((0,), (1,)), (()...  60.5 us
    reduce_sum x2, other arithmetic, attend_block(): weight_sum = weight_sum * shrink + jnp.sum(weights, axis=2)  55.2 us
    psum x1, blocking collectives, body(): lax.psum((local_sum(guided), local_sum(guided * guided), local_sum(condit...  28.4 us
    all_gather x1, local copies, waits for them, and re-layouts, body(): key_rows = lax.all_gather(keys[0], 'seq', axis=0, tiled=True)  25.5 us
  transfers between devices with their start and end apart: 4, of which 4 were waited for; matrix products, arithmetic and copies ran while one was open for 28% of the time, Pallas kernels for 0%

commit v1 on v0

--- a/solution.py
+++ b/solution.py
@@ -1,13 +1,31 @@
+import functools
 import jax
 import jax.numpy as jnp
 from jax import lax
 from jax.sharding import PartitionSpec as P
+from jax.lax import axis_index, axis_size, ppermute
 
 HEAD_DIM = 128
 FRAME_SLOTS = 480
 GUIDANCE = 5.0
 RESCALE = 0.7
 NEGATIVE = -1e30
+
+
+def create_lines_here(q_in, mesh_ax):
+    shares = axis_size(mesh_ax)
+    right_arr = sorted(((rr, (rr + 1) % shares) for rr in range(shares)))
+    oldest = q_in
+    sides = [oldest]
+    for q in [*range(1, shares)]:
+        oldest = ppermute(oldest, mesh_ax, right_arr)
+        sides.insert(0, oldest)
+    prior = jnp.concatenate(sides, 0)
+    f_next = axis_index(mesh_ax) + 1
+    return jnp.roll(prior, f_next * q_in.shape[0], 0)
+
+
+expand_area_for = functools.partial(create_lines_here, mesh_ax="seq")
 
 
 def frame_valid(positions, counts_table):
@@ -55,7 +73,7 @@
         jnp.zeros((head_count, row_count, HEAD_DIM), jnp.float32),
     )
     text_state = attend_block(empty_state, text_keys[0], text_values[0], query_heads, text_mask)
-    key_rows = lax.all_gather(keys[0], "seq", axis=0, tiled=True)
+    key_rows = expand_area_for(keys[0])
     value_rows = lax.all_gather(values[0], "seq", axis=0, tiled=True)
     positions = jnp.arange(key_rows.shape[0], dtype=jnp.int32)
     row_max, weight_sum, mixed_sum = attend_block(

time: 639 us -> 924 us (1.45)
  waiting for transfers between devices: 292 us -> 475 us
  local copies, waits for them, and re-layouts: 65.8 us -> 160 us
    ppermute x0 -> x7, waiting for transfers between devices: none -> 328 us  [create_lines_here(): oldest = ppermute(oldest, mesh_ax, right_arr)]
    all_gather x1 -> x0, waiting for transfers between devices: 141 us -> none  [body(): key_rows = lax.all_gather(keys[0], 'seq', axis=0, tiled=True)]
    concatenate x0 -> x1, local copies, waits for them, and re-layouts: none -> 60.8 us  [create_lines_here(): return jnp.roll(prior, f_next * q_in.shape[0], 0)]
    ppermute x0 -> x7, local copies, waits for them, and re-layouts: none -> 30.6 us  [create_lines_here(): oldest = ppermute(oldest, mesh_ax, right_arr)]
    all_gather x1 -> x0, local copies, waits for them, and re-layouts: 25.5 us -> none  [body(): key_rows = lax.all_gather(keys[0], 'seq', axis=0, tiled=True)]
    all_gather x1, waiting for transfers between devices: 24.8 us -> 0.01 us  [body(): value_rows = lax.all_gather(values[0], 'seq', axis=0, tiled=True)]
    reduce_scatter x1, waiting for transfers between devices: 60.5 us -> 81.9 us  [body(): lax.psum_scatter(lax.dot_general(out_weight, attended, (((0,), (1,)), (()...]
    dynamic_slice x0 -> x1, local copies, waits for them, and re-layouts: none -> 19.2 us  [create_lines_here(): return jnp.roll(prior, f_next * q_in.shape[0], 0)]
  transfers between devices with their start and end apart: 4 -> 10, of which waited for: 4 -> 8; matrix products, arithmetic and copies ran while one was open for 28% -> 29% of each run, Pallas kernels for 0% -> 0%
where the time goes in v1:
time: 924 us; the launch traced here: 916 us
  waiting for transfers between devices  475 us (51%)
  matrix products  163 us (18%)
  local copies, waits for them, and re-layouts  160 us (17%)
  other arithmetic  59 us (6%)
  blocking collectives  41.9 us (5%)
  between operations  15.2 us (2%)
    ppermute x7, waiting for transfers between devices, create_lines_here(): oldest = ppermute(oldest, mesh_ax, right_arr)  328 us
    reduce_scatter x1, waiting for transfers between devices, body(): lax.psum_scatter(lax.dot_general(out_weight, attended, (((0,), (1,)), (()...  81.9 us
    dot_general x2, matrix products, attend_block(): jnp.einsum('qhd,khd->hqk', query_heads, key_heads, preferred_element_type...  69.2 us
    dot_general x2, matrix products, attend_block(): jnp.einsum('hqk,khd->hqd', weights.astype(jnp.bfloat16), value_heads, pre...  65.9 us
    all_gather x1, waiting for transfers between devices, body(): gathered = lax.all_gather(branch, 'cfg', axis=0, tiled=True)  65.1 us
    concatenate x1, local copies, waits for them, and re-layouts, create_lines_here(): return jnp.roll(prior, f_next * q_in.shape[0], 0)  60.8 us
    reduce_sum x2, other arithmetic, attend_block(): weight_sum = weight_sum * shrink + jnp.sum(weights, axis=2)  54.7 us
    ppermute x7, local copies, waits for them, and re-layouts, create_lines_here(): oldest = ppermute(oldest, mesh_ax, right_arr)  30.6 us
  transfers between devices with their start and end apart: 10, of which 8 were waited for; matrix products, arithmetic and copies ran while one was open for 29% of the time, Pallas kernels for 0%

profile of v1, /device:TPU:0, one launch (start us, length us, event | category | flops | bytes accessed | tf_op | source)
XLA Modules:
  0.0 915.6 jit_solution(1224017717339372455)
XLA Ops:
  6.5 0.0 all-gather.5.cloned.1.call-start
  6.5 0.5 collective-permute-start
  7.0 31.8 %collective-permute-done = bf16[480,2560]{1,0:T(8,128)(2,1)S(1)} collective-permute-done((bf16[480,2560]{1,0:T(8,128)(2,1)}, bf16[480,2560]{1,0:T(8,128)(2,1)S(1)}, u32[]{:S(2)}, u32[]{:S(2)}) %collective-permute-start) | collective-permute-done | bytes 2457632 | tf_op jit(solution)/shard_map/ppermute | solution.py:21
  38.8 0.0 collective-permute-start.1
  38.8 0.0 all-gather.5.cloned.1.call-update
  38.9 0.0 reduce-scatter.2.cloned.1.call-start
  38.9 60.8 %collective-permute-done.1 = bf16[480,2560]{1,0:T(8,128)(2,1)} collective-permute-done((bf16[480,2560]{1,0:T(8,128)(2,1)S(1)}, bf16[480,2560]{1,0:T(8,128)(2,1)}, u32[]{:S(2)}, u32[]{:S(2)}) %collective-permute-start.1) | collective-permute-done | bytes 2457632 | tf_op jit(solution)/shard_map/ppermute | solution.py:21
  99.7 0.0 collective-permute-start.2
  99.7 84.1 %collective-permute-done.2 = bf16[480,2560]{1,0:T(8,128)(2,1)S(1)} collective-permute-done((bf16[480,2560]{1,0:T(8,128)(2,1)}, bf16[480,2560]{1,0:T(8,128)(2,1)S(1)}, u32[]{:S(2)}, u32[]{:S(2)}) %collective-permute-start.2) | collective-permute-done | bytes 2457632 | tf_op jit(solution)/shard_map/ppermute | solution.py:21
  183.8 1.5 copy-done.3
  185.3 0.0 collective-permute-start.3
  185.3 83.9 %collective-permute-done.3 = bf16[480,2560]{1,0:T(8,128)(2,1)S(1)} collective-permute-done((bf16[480,2560]{1,0:T(8,128)(2,1)S(1)}, bf16[480,2560]{1,0:T(8,128)(2,1)S(1)}, u32[]{:S(2)}, u32[]{:S(2)}) %collective-permute-start.3) | collective-permute-done | bytes 2457632 | tf_op jit(solution)/shard_map/ppermute | solution.py:21
  269.2 1.4 copy-done.4
  270.6 0.0 collective-permute-start.4
  270.6 36.4 %collective-permute-done.4 = bf16[480,2560]{1,0:T(8,128)(2,1)S(1)} collective-permute-done((bf16[480,2560]{1,0:T(8,128)(2,1)S(1)}, bf16[480,2560]{1,0:T(8,128)(2,1)S(1)}, u32[]{:S(2)}, u32[]{:S(2)}) %collective-permute-start.4) | collective-permute-done | bytes 2457632 | tf_op jit(solution)/shard_map/ppermute | solution.py:21
  307.1 1.5 copy-done.5
  308.6 0.0 collective-permute-start.5
  308.6 31.2 %collective-permute-done.5 = bf16[480,2560]{1,0:T(8,128)(2,1)} collective-permute-done((bf16[480,2560]{1,0:T(8,128)(2,1)S(1)}, bf16[480,2560]{1,0:T(8,128)(2,1)}, u32[]{:S(2)}, u32[]{:S(2)}) %collective-permute-start.5) | collective-permute-done | bytes 2457632 | tf_op jit(solution)/shard_map/ppermute | solution.py:21
  339.8 0.0 collective-permute-start.6
  340.4 1.3 dynamic-slice
  341.8 0.8 dynamic-update-slice
  342.6 13.5 %all-reduce = s32[8]{0:T(128)S(1)} all-reduce(s32[8]{0:T(128)S(1)} %dynamic-update-slice), channel_id=1, replica_groups=mesh['cfg'=2,'seq'=8,'tp'=2] {'seq'}, use_global_device_ids=true, to_apply=%add | all-reduce | flops 8 | bytes 64
  356.1 4.4 copy.58
  360.5 0.0 copy-done.2
  360.5 2.9 copy.52
  364.1 4.4 copy.53
  368.5 4.4 copy.56
  373.0 0.0 copy-done.6
  373.0 0.1 select_reduce_fusion
  373.1 12.0 %fusion.6 = (f32[20,480]{1,0:T(8,128)S(1)}, f32[20,480,512]{2,1,0:T(8,128)}) fusion(pred[512]{0:T(512)(128)(4,1)S(1)} %iota_compare_fusion.2, bf16[480,20,128]{0,2,1:T(8,128)(2,1)S(1)} %bitcast.100, bf16[512,20,128]{0,2,1:T(8,128)(2,1)} %bitcast.105), kind=kOutput, calls=%fused_computation.10 | convolution fusion | flops 1273027200 | bytes 24778752 | tf_op jit(solution)/shard_map/qhd,khd->hqk/dot_general | solution.py:46
  385.1 4.4 copy.66
  389.5 4.4 copy.65
  393.8 4.4 copy.64
  398.2 4.4 copy.63
  402.6 4.4 copy.62
  407.0 4.4 copy.61
  411.3 0.0 collective-permute-done.6
  411.3 4.3 copy.60
  415.7 60.8 %concatenate.6 = bf16[7680,2560]{0,1:T(8,128)(2,1)} concatenate(bf16[480,2560]{0,1:T(8,128)(2,1)} %copy.60, bf16[480,2560]{0,1:T(8,128)(2,1)} %copy.61, bf16[480,2560]{0,1:T(8,128)(2,1)} %copy.62, bf16[480,2560]{0,1:T(8,128)(2,1)} %copy.63, bf16[480,2560]{0,1:T(8,128)(2,1)} %copy.64, bf16[480,2560]{0,1:T(8,128)(2,1)} %copy.65, bf16[480,2560]{0,1:T(8,128)(2,1)} %copy.66, ...), dimensions={0} | concatenate | bytes 78643200 | tf_op jit(solution)/shard_map/jit(_roll_dynamic)/concatenate | solution.py:25
  476.4 19.2 %constant_dynamic-slice_fusion = bf16[3840,2560]{0,1:T(8,128)(2,1)} fusion(bf16[7680,2560]{0,1:T(8,128)(2,1)} %concatenate.6, s32[]{:T(128)S(6)} %select_n.75), kind=kLoop, calls=%fused_computation.78 | loop fusion | bytes 39321604 | tf_op jit(solution)/shard_map/jit(_roll_dynamic)/dynamic_slice | solution.py:25
  495.7 57.2 %bitcast_reduce_fusion = (f32[20,480]{1,0:T(8,128)S(1)}, f32[20,3840,480]{1,2,0:T(8,128)}) fusion(pred[3840]{0:T(1024)(128)(4,1)S(1)} %fusion.37, bf16[3840,20,128]{0,2,1:T(8,128)(2,1)} %bitcast.99, bf16[480,20,128]{0,2,1:T(8,128)(2,1)S(1)} %bitcast.101), kind=kOutput, calls=%fused_computation.1 | convolution fusion | flops 9547766784 | bytes 169616640 | tf_op jit(solution)/shard_map/qhd,khd->hqk/dot_general | solution.py:46
  552.9 9.8 %fusion.7 = f32[20,480]{1,0:T(8,128)S(1)} fusion(f32[20,480,512]{2,1,0:T(8,128)} %get-tuple-element.19, f32[20,480]{1,0:T(8,128)S(1)} %get-tuple-element.13, pred[512]{0:T(512)(128)(4,1)S(1)} %iota_compare_fusion.2), kind=kLoop, calls=%fused_computation.11 | loop fusion | flops 19651200 | bytes 19738112 | tf_op jit(solution)/shard_map/reduce_sum | solution.py:53
  562.7 0.0 copy-start.1
  562.7 45.0 %fusion.1 = f32[20,480]{1,0:T(8,128)S(1)} fusion(f32[20,3840,480]{1,2,0:T(8,128)} %get-tuple-element.17, f32[20,480]{1,0:T(8,128)S(1)} %get-tuple-element.12, pred[3840]{0:T(1024)(128)(4,1)S(1)} %fusion.37), kind=kLoop, calls=%fused_computation.4 | loop fusion | flops 147446400 | bytes 147536640 | tf_op jit(solution)/shard_map/reduce_sum | solution.py:53
  607.7 0.0 copy-done.1
  607.7 10.3 %fusion.9 = f32[20,480,128]{2,1,0:T(8,128)} fusion(bf16[512,20,128]{0,2,1:T(8,128)(2,1)S(1)} %bitcast.111, f32[20,480,512]{2,1,0:T(8,128)} %get-tuple-element.19, f32[20,480]{1,0:T(8,128)S(1)} %get-tuple-element.13, pred[512]{0:T(512)(128)(4,1)S(1)} %iota_compare_fusion.2), kind=kOutput, calls=%fused_computation.13 | convolution fusion | flops 1277952000 | bytes 27236352 | tf_op jit(solution)/shard_map/hqk,khd->hqd/dot_general | solution.py:54
  618.0 24.1 %copy.76 = bf16[1,3840,2560]{1,2,0:T(8,128)(2,1)} copy(bf16[1,3840,2560]{2,1,0:T(8,128)(2,1)} %all-gather.5.cloned.1.call-done) | data formatting | bytes 39321600 | tf_op jit(solution)/shard_map/all_gather | solution.py:77
  642.1 55.6 %fusion.17 = bf16[480,20,128]{2,0,1:T(8,128)(2,1)} fusion(f32[20,480,128]{2,1,0:T(8,128)} %fusion.9, f32[480,20]{0,1:T(8,128)S(1)} %get-tuple-element.9, f32[480,20]{0,1:T(8,128)S(1)} %get-tuple-element.10, f32[480,20]{0,1:T(8,128)S(1)} %get-tuple-element.11, bf16[3840,20,128]{0,2,1:T(8,128)(2,1)} %bitcast.104, f32[20,3840,480]{1,2,0:T(8,128)} %get-tuple-element.17, ...), kind=kOutput, calls=%fused_computation.22 | convolution fusion | flops 9590784000 | bytes 174647040 | tf_op jit(solution)/shard_map/hqk,khd->hqd/dot_general | solution.py:54
  697.7 2.9 copy.78
  700.6 19.7 %fusion.15 = bf16[5120,480]{0,1:T(8,128)(2,1)} fusion(bf16[480,2560]{0,1:T(8,128)(2,1)S(1)} %bitcast.112, bf16[2560,5120]{1,0:T(8,128)(2,1)} %param.15), kind=kOutput, calls=%fused_computation.19 | convolution fusion | flops 12585369600 | bytes 33587200 | tf_op jit(solution)/shard_map/dot_general | solution.py:89
  720.4 0.0 reduce-scatter.2.cloned.1.call-update
  720.4 0.0 all-gather.7.cloned.1.call-start
  720.4 81.9 %reduce-scatter.2.cloned.1.call-done = bf16[2560,480]{0,1:T(8,128)(2,1)} async-done(((bf16[5120,480]{0,1:T(8,128)(2,1)}), bf16[2560,480]{0,1:T(8,128)(2,1)}) %reduce-scatter.2.cloned.1.call-update) | async-done | bytes 2457616 | tf_op jit(solution)/shard_map/reduce_scatter | solution.py:88
  802.4 0.0 all-gather.7.cloned.1.call-update
  802.4 0.0 copy-done.7
  802.4 0.7 reduce_sum.49
  803.7 65.1 %all-gather.7.cloned.1.call-done = bf16[960,2560]{1,0:T(8,128)(2,1)} async-done(((bf16[480,2560]{1,0:T(8,128)(2,1)}), bf16[960,2560]{1,0:T(8,128)(2,1)}) %all-gather.7.cloned.1.call-update) | async-done | bytes 4915216 | tf_op jit(solution)/shard_map/all_gather | solution.py:101
  868.8 1.7 convolution_reduce_fusion
  870.5 2.4 fusion.28
  873.0 2.9 fusion.29
  875.9 0.0 copy-done
  875.9 1.4 fusion.30
  877.3 28.4 %all-reduce.1 = (f32[1280]{0:T(1024)S(1)}, f32[1280]{0:T(1024)S(1)}, f32[1280]{0:T(1024)S(1)}, f32[1280]{0:T(1024)S(1)}) all-reduce(f32[1280]{0:T(1024)S(1)} %fusion.30, f32[1280]{0:T(1024)S(1)} %convolution_reduce_fusion, f32[1280]{0:T(1024)S(1)} %fusion.28, f32[1280]{0:T(1024)S(1)} %fusion.29), channel_id=1, replica_groups=mesh['cfg'=2,'seq'=8,'tp'=2] {'seq'}, use_global_device_ids=true, to_apply=%region_10.11 | all-reduce | flops 5120 | bytes 40960 | tf_op jit(solution)/shard_map/psum | solution.py:113
  905.7 3.4 add_convert_fusion
  (17 shorter events, 0.1 us)
Async XLA Ops:
  6.5 611.5 %all-gather.5.cloned.1.call-start = ((), (), s32[]{:S(2)}) async-start(), calls=%async_computation.2 | async-start | bytes 22118400 | tf_op jit(solution)/shard_map/all_gather | solution.py:77
  6.5 32.3 %collective-permute-start = (bf16[480,2560]{1,0:T(8,128)(2,1)}, bf16[480,2560]{1,0:T(8,128)(2,1)S(1)}, u32[]{:S(2)}, u32[]{:S(2)}) collective-permute-start(bf16[480,2560]{1,0:T(8,128)(2,1)} %bitcast.114), channel_id=1, source_target_pairs={{0,2},{2,4},{4,6},{6,8},{8,10},{10,12},{12,14},{14,0},{1,3},{3,5},... | collective-permute-start | bytes 7372808 | tf_op jit(solution)/shard_map/ppermute | solution.py:21
  38.8 321.6 %copy-start.2 = (bf16[480,2560]{1,0:T(8,128)(2,1)}, bf16[480,2560]{1,0:T(8,128)(2,1)S(1)}, u32[]{:S(2)}) copy-start(bf16[480,2560]{1,0:T(8,128)(2,1)S(1)} %collective-permute-done) | copy-start | bytes 7372804
  38.8 60.9 %collective-permute-start.1 = (bf16[480,2560]{1,0:T(8,128)(2,1)S(1)}, bf16[480,2560]{1,0:T(8,128)(2,1)}, u32[]{:S(2)}, u32[]{:S(2)}) collective-permute-start(bf16[480,2560]{1,0:T(8,128)(2,1)S(1)} %collective-permute-done), channel_id=1, source_target_pairs={{0,2},{2,4},{4,6},{6,8},{8,10},{10,12},{12,14},{14,0},{1,3},{3,5},... | collective-permute-start | bytes 7372808 | tf_op jit(solution)/shard_map/ppermute | solution.py:21
  38.9 763.5 %reduce-scatter.2.cloned.1.call-start = ((), (), s32[]{:S(2)}) async-start(), calls=%async_computation.1 | async-start | bytes 7372800 | tf_op jit(solution)/shard_map/reduce_scatter | solution.py:88
  99.7 84.1 %collective-permute-start.2 = (bf16[480,2560]{1,0:T(8,128)(2,1)}, bf16[480,2560]{1,0:T(8,128)(2,1)S(1)}, u32[]{:S(2)}, u32[]{:S(2)}) collective-permute-start(bf16[480,2560]{1,0:T(8,128)(2,1)} %collective-permute-done.1), channel_id=1, source_target_pairs={{0,2},{2,4},{4,6},{6,8},{8,10},{10,12},{12,14},{14,0},{1,3},{3,5},... | collective-permute-start | bytes 7372808 | tf_op jit(solution)/shard_map/ppermute | solution.py:21
  183.8 1.5 copy-start.3
  185.3 83.9 %collective-permute-start.3 = (bf16[480,2560]{1,0:T(8,128)(2,1)S(1)}, bf16[480,2560]{1,0:T(8,128)(2,1)S(1)}, u32[]{:S(2)}, u32[]{:S(2)}) collective-permute-start(bf16[480,2560]{1,0:T(8,128)(2,1)S(1)} %collective-permute-done.2), channel_id=1, source_target_pairs={{0,2},{2,4},{4,6},{6,8},{8,10},{10,12},{12,14},{14,0},{1,3},{3,5},... | collective-permute-start | bytes 7372808 | tf_op jit(solution)/shard_map/ppermute | solution.py:21
  269.2 1.4 copy-start.4
  270.6 36.4 %collective-permute-start.4 = (bf16[480,2560]{1,0:T(8,128)(2,1)S(1)}, bf16[480,2560]{1,0:T(8,128)(2,1)S(1)}, u32[]{:S(2)}, u32[]{:S(2)}) collective-permute-start(bf16[480,2560]{1,0:T(8,128)(2,1)S(1)} %collective-permute-done.3), channel_id=1, source_target_pairs={{0,2},{2,4},{4,6},{6,8},{8,10},{10,12},{12,14},{14,0},{1,3},{3,5},... | collective-permute-start | bytes 7372808 | tf_op jit(solution)/shard_map/ppermute | solution.py:21
  307.1 1.5 copy-start.5
  308.6 31.2 %collective-permute-start.5 = (bf16[480,2560]{1,0:T(8,128)(2,1)S(1)}, bf16[480,2560]{1,0:T(8,128)(2,1)}, u32[]{:S(2)}, u32[]{:S(2)}) collective-permute-start(bf16[480,2560]{1,0:T(8,128)(2,1)S(1)} %collective-permute-done.4), channel_id=1, source_target_pairs={{0,2},{2,4},{4,6},{6,8},{8,10},{10,12},{12,14},{14,0},{1,3},{3,5},... | collective-permute-start | bytes 7372808 | tf_op jit(solution)/shard_map/ppermute | solution.py:21
  339.8 71.5 %collective-permute-start.6 = (bf16[480,2560]{1,0:T(8,128)(2,1)}, bf16[480,2560]{1,0:T(8,128)(2,1)}, u32[]{:S(2)}, u32[]{:S(2)}) collective-permute-start(bf16[480,2560]{1,0:T(8,128)(2,1)} %collective-permute-done.5), channel_id=1, source_target_pairs={{0,2},{2,4},{4,6},{6,8},{8,10},{10,12},{12,14},{14,0},{1,3},{3,5},... | collective-permute-start | bytes 7372808 | tf_op jit(solution)/shard_map/ppermute | solution.py:21
  356.1 16.9 %copy-start.6 = (s32[8]{0:T(128)}, s32[8]{0:T(128)S(1)}, u32[]{:S(2)}) copy-start(s32[8]{0:T(128)S(1)} %all-reduce) | copy-start | bytes 100
  562.7 45.0 %copy-start.1 = (bf16[1,512,2560]{1,2,0:T(8,128)(2,1)S(1)}, bf16[1,512,2560]{1,2,0:T(8,128)(2,1)}, u32[]{:S(2)}) copy-start(bf16[1,512,2560]{1,2,0:T(8,128)(2,1)} %copy.56) | copy-start | bytes 7864324
  720.4 82.0 %copy-start.7 = (s32[8]{0:T(128)S(1)}, s32[8]{0:T(128)}, u32[]{:S(2)}) copy-start(s32[8]{0:T(128)} %copy-done.6) | copy-start | bytes 100
  720.4 148.4 %all-gather.7.cloned.1.call-start = ((), (), s32[]{:S(2)}) async-start(), calls=%async_computation.3 | async-start | bytes 7372800 | tf_op jit(solution)/shard_map/all_gather | solution.py:101
  868.8 7.1 copy-start
Sparse Core Ops, SparseCore 0:
  39.0 246.1 all-gather.4
  720.5 81.8 reduce-scatter.1
  803.9 64.8 all-gather.6
